TPU v7x, 32 devices: a whole 2x2x4 slice. The times are simulated.
32 devices in a mesh: beam: 8 (over y, x, core), hid: 4 (over z).
Axes of the slice: x: 2, y: 2, z: 4, core: 2. Of those that a mesh axis runs over, the one named last changes fastest.
Arguments:
- queries: bfloat16 [512, 256], P('beam'), may hold values from -6 to 6
- beam_ids: int32 [512, 256], P('beam'), may hold values from 0 to 131071, as said below
- child_table: bfloat16 [262144, 256], P('beam'), may hold values from -6 to 6
- w_query: bfloat16 [256, 1024], P(None, 'hid'), may hold values from -0.21875 to 0.21875
- w_child: bfloat16 [256, 1024], P(None, 'hid'), may hold values from -0.21875 to 0.21875
- w_cross: bfloat16 [256, 1024], P(None, 'hid'), may hold values from -0.21875 to 0.21875
- bias: float32 [1024], P('hid'), may hold values from -3 to 3
- w_out: float32 [1024], P('hid'), may hold values from -0.1875 to 0.1875
Outputs:
- scores: float32 [512, 512], P('beam', 'hid')
Inputs may be any that keep to these rules, and one draw needn't show every extreme that they name: `beam_ids`: each id b names a node of the current level; its children are rows 2 b and 2 b + 1 of child_table. Among the ids of one index of beam's 64 queries, at most 3072 lie in the rows held by one index of beam (ids r * 16384 to (r + 1) * 16384 - 1 for index r), and in every draw one such index receives exactly 3072 from every index of beam.
All inputs are finite; a program needn't handle non-finite values.
Results may differ from a plain program's by a relative error of at most 0.0019.
Values may be sent and summed in bfloat16 or wider, within the bound.
No kernel may reach another device: no remote copies, remote signals or barrier semaphores. Data moves between devices by JAX's collectives and lax.ppermute only.
A program may use at most 128 MiB of HBM per device.

v0:
```python
import functools

import jax
import jax.numpy as jnp
from jax import lax
from jax.experimental import pallas as pl
from jax.experimental.pallas import tpu as pltpu
from jax.sharding import PartitionSpec as P

LANES = 128
TILES = 32
DIGITS = 3
ROWS = 128
OUT_SLOTS = 8
IN_SLOTS = 4
PIECE = 640


def iota(shape, dim):
    return lax.broadcasted_iota(jnp.int32, shape, dim)


def dot(a, b):
    return jnp.dot(a, b, preferred_element_type=jnp.float32)


def aligned(index, size):
    return pl.ds(pl.multiple_of(index, size), size)


def doubler():
    return (iota((2 * ROWS, ROWS), 0) >> 1 == iota((2 * ROWS, ROWS), 1)).astype(jnp.float32).astype(jnp.bfloat16)


def fetch_kernel(
    slots, embed, me_ref, x_ref, table_hbm,
    chunks_hbm, used_ref, name_ref, gidx,
    table, table_sem, eighths, insides, most_v, most_s, most_sem, rows_v, rows_sem, names_v, name_s, name_sem,
    q2f, work, work_sem, *rows_s,
):
    queries = x_ref.shape[0]
    blocks = queries // 8
    half = table_hbm.shape[0] * 4
    table_copy = pltpu.make_async_copy(table_hbm, table, table_sem)
    table_copy.start()

    lane = iota((ROWS, LANES), 1)
    lane8 = iota((8, LANES), 1)
    pick_row, pick_lane = iota((DIGITS * slots, LANES), 0), iota((DIGITS * slots, LANES), 1)
    spread = jnp.zeros((DIGITS * slots, LANES), jnp.float32)
    for digit in range(DIGITS):
        spread = jnp.where(pick_row == (pick_lane >> 1) + digit * slots, 256.0**digit, spread)
    spread = jnp.where(pick_lane < 2 * slots, spread, 0.0).astype(jnp.bfloat16)
    from_lane, to_lane = iota((LANES, LANES), 0), iota((LANES, LANES), 1)
    before = ((from_lane & 1) == 0) & ((from_lane >> 1) < (to_lane >> 1))
    before = before.astype(jnp.float32).astype(jnp.bfloat16)
    base = (me_ref[0] * half).astype(jnp.float32)
    twice = doubler()

    def compact(step, most):
        here = aligned(step * ROWS, ROWS)
        local = dot(x_ref[here, embed:], spread) - base
        owned = (local >= 0.0) & (local < float(half)) & (lane < 2 * slots)
        first = owned & ((lane & 1) == 0)
        mark = jnp.where(first, 1.0, 0.0)
        rank = dot(mark.astype(jnp.bfloat16), before).astype(jnp.int32)
        gidx[here, :] = jnp.where(owned, rank, -1)
        moved = jnp.where(first, ((lane - rank) << 16) + local.astype(jnp.int32), 0)
        for bit in range(7):
            other = pltpu.roll(moved, LANES - 2**bit, axis=1)
            flag = 65536 << bit
            moved = jnp.where((other & flag) != 0, other, jnp.where((moved & flag) != 0, 0, moved))
        total = jnp.broadcast_to(jnp.sum(mark, axis=1, keepdims=True), (ROWS, LANES)).astype(jnp.int32)
        eighth, inside = (moved & 65535) >> 2, (moved & 3) << 1
        for i in range(ROWS // 8):
            block = step * (ROWS // 8) + i
            to = aligned(block << 7, LANES)
            part = slice(i * 8, (i + 1) * 8)
            eighths[:, to] = eighth[part]
            insides[:, to] = inside[part] + (((block << 7) + lane8) << 3)
            most = jnp.where(lane8 == block, jnp.max(total[part], axis=0, keepdims=True), most)
        q2f[aligned(step * 2 * ROWS, 2 * ROWS), :] = dot(twice, x_ref[here, :embed])
        return most

    most_v[...] = lax.fori_loop(0, queries // ROWS, compact, jnp.zeros((8, LANES), jnp.int32))
    most_copy = pltpu.make_async_copy(most_v, most_s, most_sem)
    most_copy.start()
    most_copy.wait()

    zero = jnp.zeros((8, LANES), jnp.int32)

    def append(block, carry):
        used, held = carry
        more = most_s[0, block]
        turn, low = used & (LANES - 1), used >> 7
        crossed = turn + more >= LANES
        kept = []
        for source, target, last in zip((eighths, insides), (rows_v, names_v), held):
            rolled = pltpu.roll(source[:, aligned(block << 7, LANES)], turn, axis=1)
            merged = jnp.where(lane8 >= turn, rolled, last)
            target[:, aligned(low << 7, LANES)] = merged
            kept.append(jnp.where(crossed, rolled, merged))
        return used + more, tuple(kept)

    used, held = lax.fori_loop(0, blocks, append, (0, (zero, zero)), unroll=8)
    for target, last in zip((rows_v, names_v), held):
        target[:, aligned((used >> 7) << 7, LANES)] = last
    chunks = (used + TILES - 1) >> (TILES.bit_length() - 1)
    used_ref[0] = chunks
    name_ref[...] = names_v[0:1, :]

    def scalar_copies(act):
        for start in range(0, names_v.shape[1], PIECE):
            here = pl.ds(start, min(PIECE, names_v.shape[1] - start))

            @pl.when(start < chunks * TILES)
            def _():
                for s in range(8):
                    act(pltpu.make_async_copy(rows_v.at[pl.ds(s, 1), here], rows_s[s].at[:, here], rows_sem.at[s]))
                act(pltpu.make_async_copy(names_v.at[pl.ds(0, 1), here], name_s.at[:, here], name_sem))

    scalar_copies(lambda copy: copy.start())
    scalar_copies(lambda copy: copy.wait())
    table_copy.wait()

    pair = iota((8, LANES), 0) >> 1
    child = iota((8, LANES), 0) & 1

    def out_copy(number):
        slot = number & (OUT_SLOTS - 1)
        return pltpu.make_async_copy(work.at[slot], chunks_hbm.at[number], work_sem.at[slot])

    def chunk(number, carry):
        slot = number & (OUT_SLOTS - 1)

        @pl.when(number >= OUT_SLOTS)
        def _():
            out_copy(number - OUT_SLOTS).wait()

        def tile(t, carry):
            at = number * TILES + t
            block = name_s[0, at] >> 10
            names = names_v[:, aligned((at >> 7) << 7, LANES)]
            starts = jnp.take_along_axis(names, jnp.broadcast_to(at & (LANES - 1), (8, LANES)), axis=1) & 7
            halves = []
            for part in range(2):
                place = jnp.take_along_axis(starts, pair + 4 * part, axis=0) + child
                got = [None] * (embed // LANES)
                for s in range(4):
                    eight = table[rows_s[part * 4 + s][0, at]].astype(jnp.float32)
                    for j in range(embed // LANES):
                        piece = jnp.take_along_axis(eight[:, j * LANES : (j + 1) * LANES], place, axis=0)
                        got[j] = piece if s == 0 else jnp.where(pair == s, piece, got[j])
                halves.append(jnp.concatenate(got, axis=1))
            rows = jnp.concatenate(halves, axis=0)
            here = aligned(t << 4, 16)
            work[slot, here, :embed] = rows.astype(jnp.bfloat16)
            work[slot, here, embed:] = (rows * q2f[aligned(block << 4, 16), :]).astype(jnp.bfloat16)
            return carry

        lax.fori_loop(0, TILES, tile, 0, unroll=TILES)
        out_copy(number).start()
        return carry

    lax.fori_loop(0, chunks, chunk, 0)

    def drain(number, carry):
        out_copy(number).wait()
        return carry

    lax.fori_loop(jnp.maximum(chunks - OUT_SLOTS, 0), chunks, drain, 0)


def fetch(me, x, table, slots, embed):
    queries = x.shape[0]
    blocks = queries // 8
    tiles = -(-(blocks * slots + 2 * LANES) // LANES) * LANES
    vmem = pl.BlockSpec(memory_space=pltpu.VMEM)
    smem = pl.BlockSpec(memory_space=pltpu.SMEM)
    anywhere = pl.BlockSpec(memory_space=pl.ANY)
    i32 = jnp.int32
    return pl.pallas_call(
        functools.partial(fetch_kernel, slots, embed),
        out_shape=(
            jax.ShapeDtypeStruct((blocks * slots // TILES, TILES * 16, 2 * embed), jnp.bfloat16),
            jax.ShapeDtypeStruct((1,), i32),
            jax.ShapeDtypeStruct((1, tiles), i32),
            jax.ShapeDtypeStruct((queries, LANES), i32),
        ),
        in_specs=[smem, vmem, anywhere],
        out_specs=(anywhere, smem, vmem, vmem),
        scratch_shapes=[
            pltpu.VMEM(table.shape, table.dtype),
            pltpu.SemaphoreType.DMA(()),
            pltpu.VMEM((8, blocks * LANES), i32),
            pltpu.VMEM((8, blocks * LANES), i32),
            pltpu.VMEM((8, LANES), i32),
            pltpu.SMEM((8, LANES), i32),
            pltpu.SemaphoreType.DMA(()),
            pltpu.VMEM((8, tiles), i32),
            pltpu.SemaphoreType.DMA((8,)),
            pltpu.VMEM((8, tiles), i32),
            pltpu.SMEM((1, tiles), i32),
            pltpu.SemaphoreType.DMA(()),
            pltpu.VMEM((2 * queries, embed), jnp.float32),
            pltpu.VMEM((OUT_SLOTS, TILES * 16, 2 * embed), jnp.bfloat16),
            pltpu.SemaphoreType.DMA((OUT_SLOTS,)),
        ]
        + [pltpu.SMEM((1, tiles), i32)] * 8,
        cost_estimate=pl.CostEstimate(flops=2 * 10**10, bytes_accessed=4 * 10**7, transcendentals=0),
        name="fetch",
    )(me, x, table)


def score_kernel(embed, used_ref, names_s, x_ref, gidx, chunks_hbm, *rest):
    count = len(rest) - 7
    weights = rest[:count]
    out_ref, held, held_sem, qp2, work, work_sem, scores = rest[count:]
    queries = x_ref.shape[0]
    hidden = weights[0].shape[1]
    copies = [pltpu.make_async_copy(weights[k], held.at[k], held_sem.at[k]) for k in range(count)]
    for copy in copies:
        copy.start()
    chunks = used_ref[0]

    def in_copy(number):
        slot = number & (IN_SLOTS - 1)
        return pltpu.make_async_copy(chunks_hbm.at[number], work.at[slot], work_sem.at[slot])

    for number in range(IN_SLOTS - 1):

        @pl.when(number < chunks)
        def _():
            in_copy(number).start()

    for copy in copies:
        copy.wait()

    twice = doubler()

    def project(step, carry):
        here = aligned(step * 2 * ROWS, 2 * ROWS)
        doubled = dot(twice, x_ref[aligned(step * ROWS, ROWS), :embed]).astype(jnp.bfloat16)
        for k in range(count):
            last = held[k, 3 * embed :, :].astype(jnp.float32)
            bias = last[0:1] + last[1:2] + last[2:3]
            qp2[here, k * hidden : (k + 1) * hidden] = dot(doubled, held[k, 2 * embed : 3 * embed, :]) + bias
        return carry

    lax.fori_loop(0, queries // ROWS, project, 0)

    lane16 = iota((16, LANES), 1)

    def score_chunk(number, carry):
        ahead = number + IN_SLOTS - 1

        @pl.when(ahead < chunks)
        def _():
            in_copy(ahead).start()

        in_copy(number).wait()
        rows = work.at[number & (IN_SLOTS - 1)]
        sums = [None] * TILES
        for k in range(count):
            last = held[k, 3 * embed :, :].astype(jnp.float32)
            scale = last[3:4] + last[4:5] + last[5:6]
            pre = dot(rows[...], held[k, : 2 * embed, :])
            for t in range(TILES):
                block = names_s[0, number * TILES + t] >> 10
                own = qp2[aligned(block << 4, 16), k * hidden : (k + 1) * hidden]
                act = jnp.maximum(pre[t * 16 : (t + 1) * 16] + own, 0.0) * scale
                for j in range(0, hidden, LANES):
                    part = act[:, j : j + LANES]
                    sums[t] = part if sums[t] is None else sums[t] + part
        for t in range(TILES):
            name = names_s[0, number * TILES + t]
            here = aligned((name >> 10) << 4, 16)
            rank = (name >> 3) & (LANES - 1)
            total = jnp.sum(sums[t], axis=1, keepdims=True)
            scores[here, :] = jnp.where(lane16 == rank, total, scores[here, :])
        return carry

    lax.fori_loop(0, chunks, score_chunk, 0)

    lane8 = iota((8, LANES), 1)

    def place(block, carry):
        here = aligned(block << 3, 8)
        index = gidx[here, :]
        safe = jnp.maximum(index, 0)
        left = jnp.take_along_axis(scores[pl.ds(block * 16, 8, stride=2), :], safe, axis=1)
        right = jnp.take_along_axis(scores[pl.ds(block * 16 + 1, 8, stride=2), :], safe, axis=1)
        out_ref[here, :] = jnp.where(index < 0, 0.0, jnp.where((lane8 & 1) == 0, left, right))
        return carry

    lax.fori_loop(0, queries // 8, place, 0, unroll=8)


def score(used, names, x, gidx, chunks, weights, embed):
    queries = x.shape[0]
    depth, hidden = weights[0].shape
    vmem = pl.BlockSpec(memory_space=pltpu.VMEM)
    smem = pl.BlockSpec(memory_space=pltpu.SMEM)
    anywhere = pl.BlockSpec(memory_space=pl.ANY)
    return pl.pallas_call(
        functools.partial(score_kernel, embed),
        out_shape=jax.ShapeDtypeStruct((queries, LANES), jnp.float32),
        in_specs=[smem, smem, vmem, vmem, anywhere] + [anywhere] * len(weights),
        out_specs=vmem,
        scratch_shapes=[
            pltpu.VMEM((len(weights), depth, hidden), jnp.bfloat16),
            pltpu.SemaphoreType.DMA((len(weights),)),
            pltpu.VMEM((2 * queries, len(weights) * hidden), jnp.float32),
            pltpu.VMEM((IN_SLOTS, TILES * 16, 2 * embed), jnp.bfloat16),
            pltpu.SemaphoreType.DMA((IN_SLOTS,)),
            pltpu.VMEM((2 * queries, LANES), jnp.float32),
        ],
        name="score",
    )(used, names, x, gidx, chunks, *weights)


def thirds(x):
    high = lax.reduce_precision(x, 8, 7)
    middle = lax.reduce_precision(x - high, 8, 7)
    low = lax.reduce_precision(x - high - middle, 8, 7)
    return [high, middle, low]


def shards(queries, beam_ids, child_table, w_query, w_child, w_cross, bias, w_out):
    nbeam, nhid = lax.axis_size("beam"), lax.axis_size("hid")
    qcount, width = beam_ids.shape
    embed = queries.shape[1]
    slots = width // nhid
    half = child_table.shape[0] // 2
    assert 2 * slots <= LANES and half <= 65536 and half * nbeam <= 256**DIGITS and qcount * nbeam <= 8 * LANES

    tail = jnp.stack(thirds(bias) + thirds(w_out) + [jnp.zeros_like(bias)] * 10).astype(jnp.bfloat16)
    own = jnp.concatenate([w_child, w_cross, w_query, tail], axis=0)
    weights = [own]
    for shift in range(1, nhid):
        weights.append(lax.ppermute(own, "hid", [(i, (i + shift) % nhid) for i in range(nhid)]))

    mine = lax.dynamic_slice_in_dim(beam_ids, lax.axis_index("hid") * slots, slots, 1)
    digits = [(mine >> (8 * digit)) & 255 for digit in range(DIGITS)]
    x = jnp.concatenate([queries] + [d.astype(jnp.bfloat16) for d in digits], axis=1)
    x = lax.all_gather(x, "beam", axis=0, tiled=True)

    me = lax.axis_index("beam").astype(jnp.int32).reshape(1)
    chunks, used, names, gidx = fetch(me, x, child_table.reshape(-1, 8, embed), slots, embed)
    found = score(used, names, x, gidx, chunks, weights, embed)[:, : 2 * slots]
    parts = lax.all_to_all(found.reshape(nbeam, qcount, 2 * slots), "beam", split_axis=0, concat_axis=0, tiled=True)
    return jnp.sum(parts, axis=0)


def solution(mesh):
    return jax.shard_map(
        shards,
        mesh=mesh,
        in_specs=(
            P("beam", None),
            P("beam", None),
            P("beam", None),
            P(None, "hid"),
            P(None, "hid"),
            P(None, "hid"),
            P("hid"),
            P("hid"),
        ),
        out_specs=P("beam", "hid"),
        check_vma=False,
    )
```

profile of v0, /device:TPU:8, one launch (start us, length us, event | category | flops | bytes accessed | tf_op | source)
XLA Modules:
  0.0 90.4 jit_solution(1387429314788480325)
XLA Ops:
  0.0 0.7 fusion.1
  0.7 0.7 fusion.3
  1.4 2.8 %concatenate.8.rest_0_ = bf16[784,256]{1,0:T(8,128)(2,1)S(1)} concatenate(bf16[256,256]{1,0:T(8,128)(2,1)} %param.12, bf16[256,256]{1,0:T(8,128)(2,1)} %param.13, bf16[256,256]{1,0:T(8,128)(2,1)} %param.11, bf16[1,256]{1,0:T(2,128)(2,1)S(1)} %stack.32, bf16[1,256]{1,0:T(2,128)(2,1)S(1)} %stack.33, bf16[1,256]{1,0:T(2,128)(2,1)S(1)} %stack.34, bf16[1,256]{1,0:T(2,128)(2,1)S(1)} %stack.35, ...), dimensions={0} | concatenate | bytes 802816 | tf_op jit(solution)/shard_map/concatenate | solution.py:338
  4.2 0.0 copy-start
  4.2 0.1 collective-permute-start.2
  4.3 3.0 %collective-permute-start.1 = (bf16[784,256]{1,0:T(8,128)(2,1)S(1)}, bf16[784,256]{1,0:T(8,128)(2,1)S(1)}, u32[]{:S(2)}, u32[]{:S(2)}) collective-permute-start(bf16[784,256]{1,0:T(8,128)(2,1)S(1)} %concatenate.8.rest_0_), channel_id=1, source_target_pairs={{0,2},{1,3},{2,0},{3,1},{4,6},{5,7},{6,4},{7,5},{8,10},{9,11},{10,... | collective-permute-start | bytes 1204232 | tf_op jit(solution)/shard_map/ppermute | solution.py:341
  7.3 2.5 %collective-permute-start = (bf16[784,256]{1,0:T(8,128)(2,1)S(1)}, bf16[784,256]{1,0:T(8,128)(2,1)S(1)}, u32[]{:S(2)}, u32[]{:S(2)}) collective-permute-start(bf16[784,256]{1,0:T(8,128)(2,1)S(1)} %concatenate.8.rest_0_), channel_id=1, source_target_pairs={{0,1},{1,2},{2,3},{3,0},{4,5},{5,6},{6,7},{7,4},{8,9},{9,10},{10,1... | collective-permute-start | bytes 1204232 | tf_op jit(solution)/shard_map/ppermute | solution.py:341
  9.8 0.8 and_convert_fusion.2
  10.6 0.8 pad_maximum_fusion
  11.5 10.9 %all_gather.3.x_ref = bf16[512,448]{1,0:T(8,128)(2,1)} all-gather(bf16[64,448]{1,0:T(8,128)(2,1)S(1)} %pad_maximum_fusion), channel_id=1, replica_groups=mesh['beam'=8,'hid'=4] {'beam'}, dimensions={0}, use_global_device_ids=true | all-gather | bytes 516096 | tf_op jit(solution)/shard_map/all_gather | solution.py:346
  22.4 16.5 %fetch.1 = (bf16[128,512,512]{2,1,0:T(8,128)(2,1)}, s32[1]{0:T(128)}, s32[1,4352]{1,0:T(1,128)}, s32[512,128]{1,0:T(8,128)}) custom-call(s32[1]{0:T(128)} %bitcast.me_ref, bf16[512,448]{1,0:T(8,128)(2,1)} %all_gather.3.x_ref, bf16[4096,8,256]{2,1,0:T(8,128)(2,1)} %bitcast.4), custom_call_target="tpu_custom_call" | custom-call | flops 20000000000 | bytes 40000000 | tf_op jit(solution)/shard_map/fetch/pallas_call | solution.py:182
  38.9 0.0 collective-permute-done.2.rest_3_
  38.9 0.0 copy-start.1
  39.0 0.0 collective-permute-done.1.rest_2_
  39.0 0.0 copy-start.2
  39.0 2.5 %collective-permute-done.rest_1_ = bf16[784,256]{1,0:T(8,128)(2,1)S(1)} collective-permute-done((bf16[784,256]{1,0:T(8,128)(2,1)S(1)}, bf16[784,256]{1,0:T(8,128)(2,1)S(1)}, u32[]{:S(2)}, u32[]{:S(2)}) %collective-permute-start) | collective-permute-done | bytes 401440 | tf_op jit(solution)/shard_map/ppermute | solution.py:341
  41.4 0.0 copy-start.3
  41.4 0.0 copy-done
  41.4 0.0 copy-done.1
  41.4 0.0 copy-done.2
  41.4 0.7 copy-done.3
  42.2 25.6 %score.1 = f32[512,128]{1,0:T(8,128)} custom-call(s32[1]{0:T(128)} %get-tuple-element.9.used_ref, s32[1,4352]{1,0:T(1,128)} %get-tuple-element.10.names_s, bf16[512,448]{1,0:T(8,128)(2,1)} %all_gather.3.x_ref, s32[512,128]{1,0:T(8,128)} %get-tuple-element.11.gidx, bf16[128,512,512]{2,1,0:T(8,128)(2,1)} %get-tuple-element.12.chunks_hbm, ...), custom_call_target="tpu_custom_call" | custom-call | tf_op jit(solution)/shard_map/score/pallas_call | solution.py:305
  67.7 22.0 %all_to_all.5 = f32[8,64,128]{2,1,0:T(8,128)S(1)} all-to-all(f32[8,64,128]{2,1,0:T(8,128)} %bitcast.3), channel_id=1, replica_groups=mesh['beam'=8,'hid'=4] {'beam'}, dimensions={0} | all-to-all | bytes 524288 | tf_op jit(solution)/shard_map/all_to_all | solution.py:351
  89.7 0.6 reduce_sum.9
  (8 shorter events, 0.0 us)
Async XLA Ops:
  4.2 37.2 %copy-start = (bf16[784,256]{1,0:T(8,128)(2,1)}, bf16[784,256]{1,0:T(8,128)(2,1)S(1)}, u32[]{:S(2)}) copy-start(bf16[784,256]{1,0:T(8,128)(2,1)S(1)} %concatenate.8.rest_0_) | copy-start | bytes 1204228
  4.2 34.7 %collective-permute-start.2 = (bf16[784,256]{1,0:T(8,128)(2,1)S(1)}, bf16[784,256]{1,0:T(8,128)(2,1)S(1)}, u32[]{:S(2)}, u32[]{:S(2)}) collective-permute-start(bf16[784,256]{1,0:T(8,128)(2,1)S(1)} %concatenate.8.rest_0_), channel_id=1, source_target_pairs={{0,3},{1,0},{2,1},{3,2},{4,7},{5,4},{6,5},{7,6},{8,11},{9,8},{10,9... | collective-permute-start | bytes 1204232 | tf_op jit(solution)/shard_map/ppermute | solution.py:341
  4.3 34.7 %collective-permute-start.1 = (bf16[784,256]{1,0:T(8,128)(2,1)S(1)}, bf16[784,256]{1,0:T(8,128)(2,1)S(1)}, u32[]{:S(2)}, u32[]{:S(2)}) collective-permute-start(bf16[784,256]{1,0:T(8,128)(2,1)S(1)} %concatenate.8.rest_0_), channel_id=1, source_target_pairs={{0,2},{1,3},{2,0},{3,1},{4,6},{5,7},{6,4},{7,5},{8,10},{9,11},{10,... | collective-permute-start | bytes 1204232 | tf_op jit(solution)/shard_map/ppermute | solution.py:341
  7.3 34.1 %collective-permute-start = (bf16[784,256]{1,0:T(8,128)(2,1)S(1)}, bf16[784,256]{1,0:T(8,128)(2,1)S(1)}, u32[]{:S(2)}, u32[]{:S(2)}) collective-permute-start(bf16[784,256]{1,0:T(8,128)(2,1)S(1)} %concatenate.8.rest_0_), channel_id=1, source_target_pairs={{0,1},{1,2},{2,3},{3,0},{4,5},{5,6},{6,7},{7,4},{8,9},{9,10},{10,1... | collective-permute-start | bytes 1204232 | tf_op jit(solution)/shard_map/ppermute | solution.py:341
  38.9 2.5 %copy-start.1 = (bf16[784,256]{1,0:T(8,128)(2,1)}, bf16[784,256]{1,0:T(8,128)(2,1)S(1)}, u32[]{:S(2)}) copy-start(bf16[784,256]{1,0:T(8,128)(2,1)S(1)} %collective-permute-done.2.rest_3_) | copy-start | bytes 1204228
  39.0 2.5 %copy-start.2 = (bf16[784,256]{1,0:T(8,128)(2,1)}, bf16[784,256]{1,0:T(8,128)(2,1)S(1)}, u32[]{:S(2)}) copy-start(bf16[784,256]{1,0:T(8,128)(2,1)S(1)} %collective-permute-done.1.rest_2_) | copy-start | bytes 1204228
  41.4 0.8 copy-start.3
where the time goes:
time: 91.5 us; the launch traced here: 90.4 us
  Pallas kernels  42.1 us (46%)
  blocking collectives  32.9 us (36%)
  starting transfers between devices  5.56 us (6%)
  other arithmetic  3.69 us (4%)
  local copies, waits for them, and re-layouts  3.57 us (4%)
  waiting for transfers between devices  2.46 us (3%)
    pallas_call x1, Pallas kernels, score(): pl.pallas_call(functools.partial(score_kernel, embed), out_shape=jax.Shap...  25.6 us
    all_to_all x1, blocking collectives, shards(): lax.all_to_all(found.reshape(nbeam, qcount, 2 * slots), 'beam', split_axi...  22 us
    pallas_call x1, Pallas kernels, fetch(): pl.pallas_call(functools.partial(fetch_kernel, slots, embed), out_shape=(...  16.5 us
    all_gather x1, blocking collectives, shards(): x = lax.all_gather(x, 'beam', axis=0, tiled=True)  10.9 us
    ppermute x3, starting transfers between devices, shards(): lax.ppermute(own, 'hid', [(i, (i + shift) % nhid) for i in range(nhid)])  5.56 us
    concatenate x1, local copies, waits for them, and re-layouts, shards(): own = jnp.concatenate([w_child, w_cross, w_query, tail], axis=0)  2.77 us
    ppermute x3, waiting for transfers between devices, shards(): lax.ppermute(own, 'hid', [(i, (i + shift) % nhid) for i in range(nhid)])  2.46 us
  transfers between devices with their start and end apart: 3, of which 1 were waited for; matrix products, arithmetic and copies ran while one was open for 2% of the time, Pallas kernels for 18%

commit v1 on v0

--- a/solution.py
+++ b/solution.py
@@ -9,7 +9,8 @@
 
 LANES = 128
 TILES = 32
-DIGITS = 3
+DIGITS = 2
+BASE = 512
 ROWS = 128
 OUT_SLOTS = 8
 IN_SLOTS = 4
@@ -49,12 +50,12 @@
     pick_row, pick_lane = iota((DIGITS * slots, LANES), 0), iota((DIGITS * slots, LANES), 1)
     spread = jnp.zeros((DIGITS * slots, LANES), jnp.float32)
     for digit in range(DIGITS):
-        spread = jnp.where(pick_row == (pick_lane >> 1) + digit * slots, 256.0**digit, spread)
+        spread = jnp.where(pick_row == (pick_lane >> 1) + digit * slots, float(BASE) ** digit, spread)
     spread = jnp.where(pick_lane < 2 * slots, spread, 0.0).astype(jnp.bfloat16)
     from_lane, to_lane = iota((LANES, LANES), 0), iota((LANES, LANES), 1)
     before = ((from_lane & 1) == 0) & ((from_lane >> 1) < (to_lane >> 1))
     before = before.astype(jnp.float32).astype(jnp.bfloat16)
-    base = (me_ref[0] * half).astype(jnp.float32)
+    base = (me_ref[0] * half).astype(jnp.float32) - sum(BASE // 2 * BASE**digit for digit in range(DIGITS))
     twice = doubler()
 
     def compact(step, most):
@@ -212,10 +213,10 @@
     )(me, x, table)
 
 
-def score_kernel(embed, used_ref, names_s, x_ref, gidx, chunks_hbm, *rest):
-    count = len(rest) - 7
+def score_kernel(embed, used_ref, name_s, x_ref, gidx, chunks_hbm, *rest):
+    count = len(rest) - 9
     weights = rest[:count]
-    out_ref, held, held_sem, qp2, work, work_sem, scores = rest[count:]
+    out_ref, held, held_sem, qp2, work, work_sem, scores, pending, sums = rest[count:]
     queries = x_ref.shape[0]
     hidden = weights[0].shape[1]
     copies = [pltpu.make_async_copy(weights[k], held.at[k], held_sem.at[k]) for k in range(count)]
@@ -247,9 +248,34 @@
             qp2[here, k * hidden : (k + 1) * hidden] = dot(doubled, held[k, 2 * embed : 3 * embed, :]) + bias
         return carry
 
-    lax.fori_loop(0, queries // ROWS, project, 0)
+    lax.fori_loop(0, queries // ROWS, project, 0, unroll=4)
 
     lane16 = iota((16, LANES), 1)
+
+    def scale_of(k):
+        last = held[k, 3 * embed :, :].astype(jnp.float32)
+        return last[3:4] + last[4:5] + last[5:6]
+
+    def activate(pre, name, k):
+        own = qp2[aligned((name >> 10) << 4, 16), k * hidden : (k + 1) * hidden]
+        act = jnp.maximum(pre + own, 0.0) * scales[k]
+        total = act[:, :LANES]
+        for j in range(LANES, hidden, LANES):
+            total = total + act[:, j : j + LANES]
+        return total
+
+    def finish(number):
+        for t in range(TILES):
+            name = name_s[0, number * TILES + t]
+            part = slice(t * 16, (t + 1) * 16)
+            total = activate(pending[part, :], name, count - 1)
+            if count > 1:
+                total = total + sums[part, :]
+            here = aligned((name >> 10) << 4, 16)
+            rank = (name >> 3) & (LANES - 1)
+            scores[here, :] = jnp.where(lane16 == rank, jnp.sum(total, axis=1, keepdims=True), scores[here, :])
+
+    scales = [scale_of(k) for k in range(count)]
 
     def score_chunk(number, carry):
         ahead = number + IN_SLOTS - 1
@@ -260,40 +286,38 @@
 
         in_copy(number).wait()
         rows = work.at[number & (IN_SLOTS - 1)]
-        sums = [None] * TILES
-        for k in range(count):
-            last = held[k, 3 * embed :, :].astype(jnp.float32)
-            scale = last[3:4] + last[4:5] + last[5:6]
+        totals = [None] * TILES
+        for k in range(count - 1):
             pre = dot(rows[...], held[k, : 2 * embed, :])
+            if k == 0:
+                finish(jnp.maximum(number - 1, 0))
             for t in range(TILES):
-                block = names_s[0, number * TILES + t] >> 10
-                own = qp2[aligned(block << 4, 16), k * hidden : (k + 1) * hidden]
-                act = jnp.maximum(pre[t * 16 : (t + 1) * 16] + own, 0.0) * scale
-                for j in range(0, hidden, LANES):
-                    part = act[:, j : j + LANES]
-                    sums[t] = part if sums[t] is None else sums[t] + part
-        for t in range(TILES):
-            name = names_s[0, number * TILES + t]
-            here = aligned((name >> 10) << 4, 16)
-            rank = (name >> 3) & (LANES - 1)
-            total = jnp.sum(sums[t], axis=1, keepdims=True)
-            scores[here, :] = jnp.where(lane16 == rank, total, scores[here, :])
+                own = activate(pre[t * 16 : (t + 1) * 16], name_s[0, number * TILES + t], k)
+                totals[t] = own if k == 0 else totals[t] + own
+        if count > 1:
+            for t in range(TILES):
+                sums[t * 16 : (t + 1) * 16, :] = totals[t]
+        pending[...] = dot(rows[...], held[count - 1, : 2 * embed, :])
         return carry
 
     lax.fori_loop(0, chunks, score_chunk, 0)
+    finish(jnp.maximum(chunks - 1, 0))
 
     lane8 = iota((8, LANES), 1)
 
-    def place(block, carry):
-        here = aligned(block << 3, 8)
-        index = gidx[here, :]
+    def place(block):
+        index = gidx[aligned(block << 3, 8), :]
         safe = jnp.maximum(index, 0)
         left = jnp.take_along_axis(scores[pl.ds(block * 16, 8, stride=2), :], safe, axis=1)
         right = jnp.take_along_axis(scores[pl.ds(block * 16 + 1, 8, stride=2), :], safe, axis=1)
-        out_ref[here, :] = jnp.where(index < 0, 0.0, jnp.where((lane8 & 1) == 0, left, right))
+        return jnp.where(index < 0, 0.0, jnp.where((lane8 & 1) == 0, left, right))
+
+    def place_two(two, carry):
+        both = jnp.concatenate([place(2 * two), place(2 * two + 1)], axis=0)
+        out_ref[aligned(two << 4, 16), :] = both.astype(out_ref.dtype)
         return carry
 
-    lax.fori_loop(0, queries // 8, place, 0, unroll=8)
+    lax.fori_loop(0, queries // 16, place_two, 0, unroll=4)
 
 
 def score(used, names, x, gidx, chunks, weights, embed):
@@ -314,16 +338,52 @@
             pltpu.VMEM((IN_SLOTS, TILES * 16, 2 * embed), jnp.bfloat16),
             pltpu.SemaphoreType.DMA((IN_SLOTS,)),
             pltpu.VMEM((2 * queries, LANES), jnp.float32),
+            pltpu.VMEM((TILES * 16, hidden), jnp.float32),
+            pltpu.VMEM((TILES * 16, LANES), jnp.float32),
         ],
         name="score",
     )(used, names, x, gidx, chunks, *weights)
 
 
-def thirds(x):
-    high = lax.reduce_precision(x, 8, 7)
-    middle = lax.reduce_precision(x - high, 8, 7)
-    low = lax.reduce_precision(x - high - middle, 8, 7)
-    return [high, middle, low]
+def prepare_kernel(slots, place_ref, queries, ids, child, cross, query, bias, scale, own, x):
+    embed = queries.shape[1]
+    for k, w in enumerate((child, cross, query)):
+        own[k * embed : (k + 1) * embed, :] = w[...]
+    row = iota((16, own.shape[1]), 0)
+    tail = jnp.zeros((16, own.shape[1]), jnp.float32)
+    for k, value in enumerate((bias, scale)):
+        left = value[...]
+        for part in range(3):
+            taken = left.astype(jnp.bfloat16).astype(jnp.float32)
+            tail = jnp.where(row == 3 * k + part, taken, tail)
+            left = left - taken
+    own[3 * embed :, :] = tail.astype(jnp.bfloat16)
+    shape = (ids.shape[1], DIGITS * slots)
+    digits = None
+    for digit in range(DIGITS):
+        value = ((ids[...] >> (digit * (BASE.bit_length() - 1))) & (BASE - 1)) - BASE // 2
+        pick = iota(shape, 0) - place_ref[0] * slots == iota(shape, 1) - digit * slots
+        pick = pick & (iota(shape, 1) >= digit * slots) & (iota(shape, 1) < (digit + 1) * slots)
+        part = dot(value.astype(jnp.float32).astype(jnp.bfloat16), pick.astype(jnp.float32).astype(jnp.bfloat16))
+        digits = part if digits is None else digits + part
+    x[:, :embed] = queries[...]
+    x[:, embed:] = digits.astype(jnp.bfloat16)
+
+
+def prepare(queries, ids, child, cross, query, bias, scale, slots):
+    embed, hidden = child.shape
+    vmem = pl.BlockSpec(memory_space=pltpu.VMEM)
+    place = lax.axis_index("hid").astype(jnp.int32).reshape(1)
+    return pl.pallas_call(
+        functools.partial(prepare_kernel, slots),
+        out_shape=(
+            jax.ShapeDtypeStruct((3 * embed + 16, hidden), jnp.bfloat16),
+            jax.ShapeDtypeStruct((queries.shape[0], embed + DIGITS * slots), jnp.bfloat16),
+        ),
+        in_specs=[pl.BlockSpec(memory_space=pltpu.SMEM)] + [vmem] * 7,
+        out_specs=(vmem, vmem),
+        name="prepare",
+    )(place, queries, ids, child, cross, query, bias.reshape(1, -1), scale.reshape(1, -1))
 
 
 def shards(queries, beam_ids, child_table, w_query, w_child, w_cross, bias, w_out):
@@ -332,17 +392,12 @@
     embed = queries.shape[1]
     slots = width // nhid
     half = child_table.shape[0] // 2
-    assert 2 * slots <= LANES and half <= 65536 and half * nbeam <= 256**DIGITS and qcount * nbeam <= 8 * LANES
-
-    tail = jnp.stack(thirds(bias) + thirds(w_out) + [jnp.zeros_like(bias)] * 10).astype(jnp.bfloat16)
-    own = jnp.concatenate([w_child, w_cross, w_query, tail], axis=0)
+    assert 2 * slots <= LANES and half <= 65536 and half * nbeam <= BASE**DIGITS and qcount * nbeam <= 8 * LANES
+
+    own, x = prepare(queries, beam_ids, w_child, w_cross, w_query, bias, w_out, slots)
     weights = [own]
     for shift in range(1, nhid):
         weights.append(lax.ppermute(own, "hid", [(i, (i + shift) % nhid) for i in range(nhid)]))
-
-    mine = lax.dynamic_slice_in_dim(beam_ids, lax.axis_index("hid") * slots, slots, 1)
-    digits = [(mine >> (8 * digit)) & 255 for digit in range(DIGITS)]
-    x = jnp.concatenate([queries] + [d.astype(jnp.bfloat16) for d in digits], axis=1)
     x = lax.all_gather(x, "beam", axis=0, tiled=True)
 
     me = lax.axis_index("beam").astype(jnp.int32).reshape(1)

time: 91.5 us -> 85.5 us (0.934)
  the two profiles are of different devices: /device:TPU:8 before, /device:TPU:0 now
where the time goes in v1:
time: 85.5 us; the launch traced here: 85.4 us
  Pallas kernels  42.9 us (50%)
  blocking collectives  29.6 us (35%)
  starting transfers between devices  6.09 us (7%)
  waiting for transfers between devices  5.27 us (6%)
  local copies, waits for them, and re-layouts  0.94 us (1%)
    pallas_call x1, Pallas kernels, score(): pl.pallas_call(functools.partial(score_kernel, embed), out_shape=jax.Shap...  24.2 us
    all_to_all x1, blocking collectives, shards(): lax.all_to_all(found.reshape(nbeam, qcount, 2 * slots), 'beam', split_axi...  18.1 us
    pallas_call x1, Pallas kernels, fetch(): pl.pallas_call(functools.partial(fetch_kernel, slots, embed), out_shape=(...  16.7 us
    all_gather x1, blocking collectives, shards(): x = lax.all_gather(x, 'beam', axis=0, tiled=True)  11.4 us
    ppermute x3, starting transfers between devices, shards(): lax.ppermute(own, 'hid', [(i, (i + shift) % nhid) for i in range(nhid)])  6.09 us
    ppermute x3, waiting for transfers between devices, shards(): lax.ppermute(own, 'hid', [(i, (i + shift) % nhid) for i in range(nhid)])  5.27 us
    pallas_call x1, Pallas kernels, prepare(): pl.pallas_call(functools.partial(prepare_kernel, slots), out_shape=(jax.S...  1.94 us
  transfers between devices with their start and end apart: 3, of which 1 were waited for; matrix products, arithmetic and copies ran while one was open for 0% of the time, Pallas kernels for 20%

profile of v1, /device:TPU:0, one launch (start us, length us, event | category | flops | bytes accessed | tf_op | source)
XLA Modules:
  0.0 85.4 jit_solution(1192195550698044085)
XLA Ops:
  0.0 1.9 %prepare.1 = (bf16[784,256]{1,0:T(8,128)(2,1)}, bf16[64,384]{1,0:T(8,128)(2,1)}) custom-call(s32[1]{0:T(128)} %bitcast.1.place_ref, bf16[64,256]{1,0:T(8,128)(2,1)} %queries.1, s32[64,256]{1,0:T(8,128)} %ids.1, bf16[256,256]{1,0:T(8,128)(2,1)} %child.1, bf16[256,256]{1,0:T(8,128)(2,1)} %cross.1, bf16[256,256]{1,0:T(8,128)(2,1)} %query.1, f32[1,256]{1,0:T(1,128)} %bitcast.7, ...), custom_call_target="tpu_custom_call" | custom-call | tf_op jit(solution)/shard_map/prepare/pallas_call | solution.py:377
  1.9 5.1 %collective-permute-start.2 = (bf16[784,256]{1,0:T(8,128)(2,1)}, bf16[784,256]{1,0:T(8,128)(2,1)S(1)}, u32[]{:S(2)}, u32[]{:S(2)}) collective-permute-start(bf16[784,256]{1,0:T(8,128)(2,1)} %get-tuple-element.16.rest_0_), channel_id=1, source_target_pairs={{0,3},{1,0},{2,1},{3,2},{4,7},{5,4},{6,5},{7,6},{8,11},{9,8},{10,9... | collective-permute-start | bytes 1204232 | tf_op jit(solution)/shard_map/ppermute | solution.py:400
  7.0 0.0 collective-permute-start.1
  7.0 1.0 %collective-permute-start = (bf16[784,256]{1,0:T(8,128)(2,1)}, bf16[784,256]{1,0:T(8,128)(2,1)S(1)}, u32[]{:S(2)}, u32[]{:S(2)}) collective-permute-start(bf16[784,256]{1,0:T(8,128)(2,1)} %get-tuple-element.16.rest_0_), channel_id=1, source_target_pairs={{0,1},{1,2},{2,3},{3,0},{4,5},{5,6},{6,7},{7,4},{8,9},{9,10},{10,1... | collective-permute-start | bytes 1204232 | tf_op jit(solution)/shard_map/ppermute | solution.py:400
  8.0 11.4 %all_gather.3.x_ref = bf16[512,384]{1,0:T(8,128)(2,1)} all-gather(bf16[64,384]{1,0:T(8,128)(2,1)} %get-tuple-element.11), channel_id=1, replica_groups=mesh['beam'=8,'hid'=4] {'beam'}, dimensions={0}, use_global_device_ids=true | all-gather | bytes 442368 | tf_op jit(solution)/shard_map/all_gather | solution.py:401
  19.5 16.7 %fetch.1 = (bf16[128,512,512]{2,1,0:T(8,128)(2,1)}, s32[1]{0:T(128)}, s32[1,4352]{1,0:T(1,128)}, s32[512,128]{1,0:T(8,128)}) custom-call(s32[1]{0:T(128)} %bitcast.me_ref, bf16[512,384]{1,0:T(8,128)(2,1)} %all_gather.3.x_ref, bf16[4096,8,256]{2,1,0:T(8,128)(2,1)} %bitcast.9), custom_call_target="tpu_custom_call" | custom-call | flops 20000000000 | bytes 40000000 | tf_op jit(solution)/shard_map/fetch/pallas_call | solution.py:183
  36.2 0.0 collective-permute-done.2.rest_3_
  36.2 0.0 copy-start
  36.2 5.3 %collective-permute-done.1.rest_2_ = bf16[784,256]{1,0:T(8,128)(2,1)S(1)} collective-permute-done((bf16[784,256]{1,0:T(8,128)(2,1)}, bf16[784,256]{1,0:T(8,128)(2,1)S(1)}, u32[]{:S(2)}, u32[]{:S(2)}) %collective-permute-start.1) | collective-permute-done | bytes 401440 | tf_op jit(solution)/shard_map/ppermute | solution.py:400
  41.5 0.0 copy-start.1
  41.5 0.0 collective-permute-done.rest_1_
  41.5 0.0 copy-start.2
  41.5 0.0 copy-done
  41.5 0.8 copy-done.1
  42.2 0.2 copy-done.2
  42.4 24.2 %score.1 = f32[512,128]{1,0:T(8,128)} custom-call(s32[1]{0:T(128)} %get-tuple-element.12.used_ref, s32[1,4352]{1,0:T(1,128)} %get-tuple-element.13.name_s, bf16[512,384]{1,0:T(8,128)(2,1)} %all_gather.3.x_ref, s32[512,128]{1,0:T(8,128)} %get-tuple-element.14.gidx, bf16[128,512,512]{2,1,0:T(8,128)(2,1)} %get-tuple-element.15.chunks_hbm, ...), custom_call_target="tpu_custom_call" | custom-call | tf_op jit(solution)/shard_map/score/pallas_call | solution.py:329
  66.7 18.1 %all_to_all.5 = f32[8,64,128]{2,1,0:T(8,128)S(1)} all-to-all(f32[8,64,128]{2,1,0:T(8,128)} %bitcast.6), channel_id=1, replica_groups=mesh['beam'=8,'hid'=4] {'beam'}, dimensions={0} | all-to-all | bytes 524288 | tf_op jit(solution)/shard_map/all_to_all | solution.py:406
  84.8 0.6 reduce_sum.9
Async XLA Ops:
  1.9 34.3 %collective-permute-start.2 = (bf16[784,256]{1,0:T(8,128)(2,1)}, bf16[784,256]{1,0:T(8,128)(2,1)S(1)}, u32[]{:S(2)}, u32[]{:S(2)}) collective-permute-start(bf16[784,256]{1,0:T(8,128)(2,1)} %get-tuple-element.16.rest_0_), channel_id=1, source_target_pairs={{0,3},{1,0},{2,1},{3,2},{4,7},{5,4},{6,5},{7,6},{8,11},{9,8},{10,9... | collective-permute-start | bytes 1204232 | tf_op jit(solution)/shard_map/ppermute | solution.py:400
  7.0 34.5 %collective-permute-start.1 = (bf16[784,256]{1,0:T(8,128)(2,1)}, bf16[784,256]{1,0:T(8,128)(2,1)S(1)}, u32[]{:S(2)}, u32[]{:S(2)}) collective-permute-start(bf16[784,256]{1,0:T(8,128)(2,1)} %get-tuple-element.16.rest_0_), channel_id=1, source_target_pairs={{0,2},{1,3},{2,0},{3,1},{4,6},{5,7},{6,4},{7,5},{8,10},{9,11},{10,... | collective-permute-start | bytes 1204232 | tf_op jit(solution)/shard_map/ppermute | solution.py:400
  7.0 34.5 %collective-permute-start = (bf16[784,256]{1,0:T(8,128)(2,1)}, bf16[784,256]{1,0:T(8,128)(2,1)S(1)}, u32[]{:S(2)}, u32[]{:S(2)}) collective-permute-start(bf16[784,256]{1,0:T(8,128)(2,1)} %get-tuple-element.16.rest_0_), channel_id=1, source_target_pairs={{0,1},{1,2},{2,3},{3,0},{4,5},{5,6},{6,7},{7,4},{8,9},{9,10},{10,1... | collective-permute-start | bytes 1204232 | tf_op jit(solution)/shard_map/ppermute | solution.py:400
  36.2 5.3 %copy-start = (bf16[784,256]{1,0:T(8,128)(2,1)}, bf16[784,256]{1,0:T(8,128)(2,1)S(1)}, u32[]{:S(2)}) copy-start(bf16[784,256]{1,0:T(8,128)(2,1)S(1)} %collective-permute-done.2.rest_3_) | copy-start | bytes 1204228
  41.5 0.8 copy-start.1
  41.5 0.9 %copy-start.2 = (bf16[784,256]{1,0:T(8,128)(2,1)}, bf16[784,256]{1,0:T(8,128)(2,1)S(1)}, u32[]{:S(2)}) copy-start(bf16[784,256]{1,0:T(8,128)(2,1)S(1)} %collective-permute-done.rest_1_) | copy-start | bytes 1204228
